TPU v7x, 32 devices: a whole 2x2x4 slice. The times are simulated.
32 devices in a mesh: row: 8 (over z, x), col: 4 (over y, core).
Axes of the slice: x: 2, y: 2, z: 4, core: 2. Of those that a mesh axis runs over, the one named last changes fastest.
Arguments:
- state: bfloat16 [256, 16384], P(None, ('row', 'col')), may hold values from -0.94921875 to 0.94921875
- adjoint: bfloat16 [256, 16384], P(None, ('col', 'row')), may hold values from -6 to 6
- features: bfloat16 [128, 16384], P(None, ('col', 'row')), may hold values from -6 to 6
- cotangent: bfloat16 [256, 16384], P(None, ('row', 'col')), may hold values from -6 to 6
- mixing: bfloat16 [256, 256], replicated, may hold values from -0.375 to 0.375
- input_weight: bfloat16 [256, 128], replicated, may hold values from -0.5 to 0.5
- tiles: bfloat16 [8, 4, 170, 128, 128], P('row', 'col'), may hold values from -0.09375 to 0.09375
- tile_rows: int32 [8, 4, 170], P('row', 'col'), may hold values from 0 to 15, as said below
- tile_cols: int32 [8, 4, 170], P('row', 'col'), may hold values from 0 to 31, as said below
- live_tiles: int32 [8, 4], P('row', 'col'), may hold values from 85 to 170, as said below
Outputs:
- new_state: bfloat16 [256, 16384], P(None, ('col', 'row'))
- new_adjoint: bfloat16 [256, 16384], P(None, ('row', 'col'))
Inputs may be any that keep to these rules, and one draw needn't show every extreme that they name: On one device the pairs (tile_rows, tile_cols) of its 170 slots are all different. `tile_cols`: see tile_rows. `live_tiles`: some device has all 170 slots live.
All inputs are finite; a program needn't handle non-finite values.
Results may differ from a plain program's by a relative error of at most 0.014.
Values may be sent and summed in bfloat16 or wider, within the bound.
No kernel may reach another device: no remote copies, remote signals or barrier semaphores. Data moves between devices by JAX's collectives and lax.ppermute only.
A program may use at most 64 MiB of HBM per device.

v0:
```python
import functools

import jax
import jax.numpy as jnp
from jax import lax
from jax.experimental import pallas as pl
from jax.experimental.pallas import tpu as pltpu
from jax.sharding import PartitionSpec as P


VMEM = pltpu.VMEM
BF16 = jnp.bfloat16
F32 = jnp.float32
NT = (((1,), (1,)), ((), ()))
TN = (((0,), (0,)), ((), ()))


def in_vmem():
    return pl.BlockSpec(memory_space=VMEM)


def swap(value, axis, size, mask):
    return lax.ppermute(value, axis, [(i, i ^ mask) for i in range(size)])


def clear_kernel(dense):
    height, width = dense.shape

    def clear(i, carry):
        dense[pl.ds(pl.multiple_of(i * 32, 32), 32), :] = jnp.zeros((32, width), dense.dtype)
        return carry

    lax.fori_loop(0, height // 32, clear, 0)


def clear(height, width):
    return pl.pallas_call(
        clear_kernel,
        out_specs=in_vmem(),
        out_shape=jax.ShapeDtypeStruct((height, width), BF16),
        compiler_params=pltpu.CompilerParams(vmem_limit_bytes=4 * 2**20),
        cost_estimate=pl.CostEstimate(flops=5 * 10**9, bytes_accessed=height * width * 2, transcendentals=0),
        name="clear",
    )()


def build_kernel(per_chunk, rows, cols, count, tiles, blank, dense):
    slots, side, _ = tiles.shape
    row_flip = lax.axis_index("col") * per_chunk
    col_flip = lax.axis_index("row") * per_chunk

    def place(slot, carry):
        r = pl.multiple_of((rows[0, 0, slot] ^ row_flip) * side, side)
        c = pl.multiple_of((cols[0, 0, slot] ^ col_flip) * side, side)
        dense[pl.ds(r, side), pl.ds(c, side)] = tiles[slot]
        return carry

    lax.fori_loop(0, jnp.clip(count[0, 0], 0, slots), place, 0)


def build(per_chunk, rows, cols, count, tiles, blank):
    smem = pl.BlockSpec(memory_space=pltpu.SMEM)
    return pl.pallas_call(
        functools.partial(build_kernel, per_chunk),
        in_specs=[smem] * 3 + [in_vmem()] * 2,
        out_specs=in_vmem(),
        out_shape=jax.ShapeDtypeStruct(blank.shape, BF16),
        input_output_aliases={4: 0},
        compiler_params=pltpu.CompilerParams(vmem_limit_bytes=4 * 2**20),
        cost_estimate=pl.CostEstimate(flops=5 * 10**9, bytes_accessed=tiles.size * 2, transcendentals=0),
        name="build",
    )(rows, cols, count, tiles, blank)


def forward_kernel(parts, extra, cuts, *refs):
    blocks, dense, rest = refs[:parts], refs[parts], refs[parts + 1 :]
    picks, rest = rest[:extra], rest[extra:]
    outs, whole = rest[:-1], rest[-1]
    width = blocks[0].shape[1]
    for k in range(parts):
        whole[:, k * width : (k + 1) * width] = blocks[k][...]
    first = 1
    if extra:
        weight, features = picks
        outs[-1][...] = jnp.dot(weight[...], features[...], preferred_element_type=F32)
        outs, first = outs[:-1], 0
    span = outs[0].shape[1]
    for j, cut in enumerate(cuts):
        start = (2 * j + first) * span
        total = jnp.dot(
            whole[...], dense[:, start : start + span], preferred_element_type=F32
        ).astype(BF16)
        height = total.shape[0] // cut
        for i in range(cut):
            outs[i][...] = total[i * height : (i + 1) * height]
        outs = outs[cut:]


def early_kernel(parts, *refs):
    blocks, dense, outs, whole = refs[:parts], refs[parts], refs[parts + 1 : -1], refs[-1]
    width = blocks[0].shape[1]
    for k in range(parts):
        whole[:, k * width : (k + 1) * width] = blocks[k][...]
    span = outs[0].shape[1]
    for j, out in enumerate(outs):
        out[...] = lax.dot_general(
            whole[...], dense[j * span : (j + 1) * span, : parts * width], NT, preferred_element_type=F32
        )


def early(blocks, dense, pieces):
    hidden, width = blocks[0].shape
    parts = len(blocks)
    span = dense.shape[0] // pieces
    return pl.pallas_call(
        functools.partial(early_kernel, parts),
        in_specs=[in_vmem()] * (parts + 1),
        out_specs=[in_vmem()] * pieces,
        out_shape=[jax.ShapeDtypeStruct((hidden, span), F32)] * pieces,
        scratch_shapes=[VMEM((hidden, parts * width), BF16)],
        compiler_params=pltpu.CompilerParams(vmem_limit_bytes=8 * 2**20),
        cost_estimate=pl.CostEstimate(flops=2 * hidden * dense.size, bytes_accessed=dense.size, transcendentals=0),
        name="backward_early",
    )(*blocks, dense)


def late_kernel(first, terms, extra, *refs):
    block, dense, rest = refs[0], refs[1], refs[2:]
    sums, picks, outs = rest[:terms], rest[terms : terms + extra], rest[terms + extra :]
    span, width = outs[0].shape[1], block.shape[1]
    for j, out in enumerate(outs):
        start = (2 * j + first) * span
        total = sums[j][...] + lax.dot_general(
            block[...], dense[start : start + span, dense.shape[1] - width :], NT, preferred_element_type=F32
        )
        if extra and j:
            total = total + picks[j - 1][...].astype(F32)
        out[...] = total.astype(BF16)


def late(block, dense, first, sums, picks):
    hidden, width = block.shape
    span = sums[0].shape[1]
    return pl.pallas_call(
        functools.partial(late_kernel, first, len(sums), len(picks)),
        in_specs=[in_vmem()] * (2 + len(sums) + len(picks)),
        out_specs=[in_vmem()] * len(sums),
        out_shape=[jax.ShapeDtypeStruct((hidden, span), BF16)] * len(sums),
        compiler_params=pltpu.CompilerParams(vmem_limit_bytes=8 * 2**20),
        cost_estimate=pl.CostEstimate(flops=hidden * dense.shape[0] * width, bytes_accessed=dense.size // 8, transcendentals=0),
    )(block, dense, *sums, *picks)


def forward(blocks, dense, picks, cuts):
    hidden, width = blocks[0].shape
    parts = len(blocks)
    span = dense.shape[1] // (2 * len(cuts))
    outs = [jax.ShapeDtypeStruct((hidden // cut, span), BF16) for cut in cuts for _ in range(cut)]
    if picks:
        outs.append(jax.ShapeDtypeStruct((hidden, span), F32))
    outs = pl.pallas_call(
        functools.partial(forward_kernel, parts, len(picks), cuts),
        in_specs=[in_vmem()] * (parts + 1 + len(picks)),
        out_specs=[in_vmem()] * len(outs),
        out_shape=outs,
        scratch_shapes=[VMEM((hidden, parts * width), BF16)],
        compiler_params=pltpu.CompilerParams(vmem_limit_bytes=8 * 2**20),
        cost_estimate=pl.CostEstimate(flops=hidden * dense.size, bytes_accessed=dense.size, transcendentals=0),
    )(*blocks, dense, *picks)
    groups = []
    for cut in cuts:
        groups.append(outs[:cut])
        outs = outs[cut:]
    return groups, outs


def join_kernel(start, *refs):
    *terms, out = refs
    height = out.shape[0]
    total = None
    for ref in terms:
        value = ref[...] if ref.shape[0] == height else ref[start : start + height, :]
        value = value.astype(F32)
        total = value if total is None else total + value
    out[...] = total.astype(BF16)


def join(terms, start=0):
    return join_call(terms, start)


def join_call(terms, start):
    return pl.pallas_call(
        functools.partial(join_kernel, start),
        in_specs=[in_vmem()] * len(terms),
        out_specs=in_vmem(),
        out_shape=jax.ShapeDtypeStruct(terms[0].shape, BF16),
        compiler_params=pltpu.CompilerParams(vmem_limit_bytes=4 * 2**20),
        cost_estimate=pl.CostEstimate(flops=10**8, bytes_accessed=2**20, transcendentals=0),
        name="join",
    )(*terms)


def state_kernel(terms, pieces, *refs):
    flow = refs[0][...].astype(F32)
    for ref in refs[1:terms]:
        flow = flow + ref[...].astype(F32)
    for i in range(terms, terms + pieces, 2):
        flow = flow + jnp.concatenate([refs[i][...], refs[i + 1][...]], axis=0).astype(F32)
    mixing, base, out = refs[terms + pieces :]
    pre = base[...] + jnp.dot(mixing[...], flow.astype(BF16), preferred_element_type=F32)
    out[...] = jnp.tanh(pre).astype(BF16)


def adjoint_kernel(terms, pieces, *refs):
    back = refs[0][...].astype(F32)
    for ref in refs[1:terms]:
        back = back + ref[...].astype(F32)
    mixing, state, cotangent, out = refs[terms:]
    pulled = lax.dot_general(mixing[...], back.astype(BF16), TN, preferred_element_type=F32)
    wide = state[...].astype(F32)
    out[...] = ((1.0 - wide * wide) * (pulled + cotangent[...].astype(F32))).astype(BF16)


def finish(kernel, terms, halves, others):
    operands = (*terms, *halves, *others)
    return pl.pallas_call(
        functools.partial(kernel, len(terms), len(halves)),
        in_specs=[in_vmem()] * len(operands),
        out_specs=in_vmem(),
        out_shape=jax.ShapeDtypeStruct(terms[0].shape, BF16),
        compiler_params=pltpu.CompilerParams(vmem_limit_bytes=4 * 2**20),
        cost_estimate=pl.CostEstimate(flops=10**9, bytes_accessed=2**21, transcendentals=0),
    )(*operands)


def per_device(state, adjoint, features, cotangent, mixing, input_weight, tiles, tile_rows, tile_cols, live_tiles):
    n_row, n_col = lax.axis_size("row"), lax.axis_size("col")
    hidden, nodes = state.shape
    slab = tiles[0, 0]
    side = slab.shape[-1]
    half_row, half_col = n_row // 2, n_col // 2

    def by_row(value, mask):
        return swap(value, "row", n_row, mask)

    def by_col(value, mask):
        return swap(value, "col", n_col, mask)

    near = [adjoint]
    for k in range(1, half_row):
        far = k > 1 and k % 2
        near.append(by_row(near[k - 1] if far else adjoint, 2 if far else 2 * k))
    adjoints = []
    for block in near:
        adjoints += [block, by_row(block, 1)]

    near = [state] + [by_col(state, 2 * k) for k in range(1, half_col)]
    states = []
    for block in near:
        states += [block, by_col(block, 1)]

    blank = clear(n_col * nodes, n_row * nodes)
    dense = build(nodes // side, tile_rows, tile_cols, live_tiles, slab, blank)

    cuts = [2 if k > 1 and k % 2 == 0 else 1 for k in range(half_row)]
    others, _ = forward(states, dense, (), cuts)
    direct = by_row(others[1][0], 2)
    crossed = {k: [by_row(part, 1) for part in others[k]] for k in range(2, half_row)}
    mine, (base,) = forward(states, dense, (input_weight, features), cuts)
    corner = join((others[0][0], direct))
    flows = [mine[0][0], by_row(mine[1][0], 2), by_row(corner, 1)]
    halves, relayed = [], None
    for k in reversed(range(2, half_row)):
        if k % 2:
            relayed = by_row(join((mine[k][0], crossed[k][0])), 2)
            continue
        last = () if relayed is None else (relayed,)
        for i in range(2):
            pair = join((mine[k][i], crossed[k][i], *last), i * hidden // 2)
            halves.append(by_row(pair, 2 * k))
        relayed = None
    new_state = finish(state_kernel, flows, halves, (mixing, base))

    sums = early(adjoints[:-1], dense, n_col)
    others = late(adjoints[-1], dense, 1, sums[1::2], ())
    others = [by_col(others[k], 1) for k in range(half_col)]
    mine = late(adjoints[-1], dense, 0, sums[::2], others[1:])
    backs = [mine[0], others[0]] + [by_col(mine[k], 2 * k) for k in range(1, half_col)]
    new_adjoint = finish(adjoint_kernel, backs, (), (mixing, state, cotangent))
    return (new_state, new_adjoint)


def solution(mesh):
    placed = (
        P(None, ("row", "col")),
        P(None, ("col", "row")),
        P(None, ("col", "row")),
        P(None, ("row", "col")),
        P(),
        P(),
        P("row", "col", None, None, None),
        P("row", "col", None),
        P("row", "col", None),
        P("row", "col"),
    )
    return jax.shard_map(
        per_device,
        mesh=mesh,
        in_specs=placed,
        out_specs=(P(None, ("col", "row")), P(None, ("row", "col"))),
        check_vma=False,
    )
```

profile of v0, /device:TPU:0, one launch (start us, length us, event | category | flops | bytes accessed | tf_op | source)
XLA Modules:
  0.0 73.7 jit_solution(14523068429351828324)
XLA Ops:
  0.7 4.1 %collective-permute-start.12 = (bf16[256,512]{1,0:T(8,128)(2,1)}, bf16[256,512]{1,0:T(8,128)(2,1)S(1)}, u32[]{:S(2)}, u32[]{:S(2)}) collective-permute-start(bf16[256,512]{1,0:T(8,128)(2,1)} %refs_0_.5), channel_id=1, source_target_pairs={{0,16},{4,20},{8,24},{12,28},{16,0},{20,4},{24,8},{28,12},{1,17},{... | collective-permute-start | bytes 786440 | tf_op jit(solution)/shard_map/ppermute | solution.py:23
  4.8 1.6 %collective-permute-start.16 = (bf16[256,512]{1,0:T(8,128)(2,1)}, bf16[256,512]{1,0:T(8,128)(2,1)S(1)}, u32[]{:S(2)}, u32[]{:S(2)}) collective-permute-start(bf16[256,512]{1,0:T(8,128)(2,1)} %refs_0_.5), channel_id=1, source_target_pairs={{0,8},{4,12},{8,0},{12,4},{16,24},{20,28},{24,16},{28,20},{1,9},{5... | collective-permute-start | bytes 786440 | tf_op jit(solution)/shard_map/ppermute | solution.py:23
  6.4 1.5 %collective-permute-start.15 = (bf16[256,512]{1,0:T(8,128)(2,1)}, bf16[256,512]{1,0:T(8,128)(2,1)S(1)}, u32[]{:S(2)}, u32[]{:S(2)}) collective-permute-start(bf16[256,512]{1,0:T(8,128)(2,1)} %refs_0_.5), channel_id=1, source_target_pairs={{0,4},{4,0},{8,12},{12,8},{16,20},{20,16},{24,28},{28,24},{1,5},{5... | collective-permute-start | bytes 786440 | tf_op jit(solution)/shard_map/ppermute | solution.py:23
  7.9 1.5 %collective-permute-start.1 = (bf16[256,512]{1,0:T(8,128)(2,1)}, bf16[256,512]{1,0:T(8,128)(2,1)S(1)}, u32[]{:S(2)}, u32[]{:S(2)}) collective-permute-start(bf16[256,512]{1,0:T(8,128)(2,1)} %refs_4_.1), channel_id=1, source_target_pairs={{0,2},{1,3},{2,0},{3,1},{4,6},{5,7},{6,4},{7,5},{8,10},{9,11},{10,... | collective-permute-start | bytes 786440 | tf_op jit(solution)/shard_map/ppermute | solution.py:23
  10.0 1.2 %clear.1.blank = bf16[2048,4096]{1,0:T(8,128)(2,1)S(1)} custom-call(), custom_call_target="tpu_custom_call" | custom-call | flops 5000000000 | bytes 16777216 | tf_op jit(solution)/shard_map/clear/pallas_call | solution.py:37
  11.3 5.8 %collective-permute-done.12.refs_4_ = bf16[256,512]{1,0:T(8,128)(2,1)S(1)} collective-permute-done((bf16[256,512]{1,0:T(8,128)(2,1)}, bf16[256,512]{1,0:T(8,128)(2,1)S(1)}, u32[]{:S(2)}, u32[]{:S(2)}) %collective-permute-start.12) | collective-permute-done | bytes 262176 | tf_op jit(solution)/shard_map/ppermute | solution.py:23
  17.0 0.7 collective-permute-start.13
  17.8 1.5 %collective-permute-start.18 = (bf16[256,512]{1,0:T(8,128)(2,1)S(1)}, bf16[256,512]{1,0:T(8,128)(2,1)S(1)}, u32[]{:S(2)}, u32[]{:S(2)}) collective-permute-start(bf16[256,512]{1,0:T(8,128)(2,1)S(1)} %collective-permute-done.12.refs_4_), channel_id=1, source_target_pairs={{0,4},{4,0},{8,12},{12,8},{16,20},{20,16},{24,28},{28,24},{1,5},{5... | collective-permute-start | bytes 786440 | tf_op jit(solution)/shard_map/ppermute | solution.py:23
  19.3 0.5 collective-permute-start.17
  19.8 2.0 %build.1.refs_4_.refs_7_.refs_1_ = bf16[2048,4096]{1,0:T(8,128)(2,1)S(1)} custom-call(s32[1,1,170]{2,1,0:T(1,128)S(1)} %copy-done.4, s32[1,1,170]{2,1,0:T(1,128)S(1)} %copy-done.5, s32[1,1]{1,0:T(1,128)S(6)} %copy.14.count, bf16[170,128,128]{2,1,0:T(8,128)(2,1)S(1)} %bitcast.3, bf16[2048,4096]{1,0:T(8,128)(2,1)S(1)} %clear.1.blank), custom_call_target="tpu_custom_call", output_to_operand_aliasing={{}: (4, {})} | custom-call | flops 5000000000 | bytes 5570560 | tf_op jit(solution)/shard_map/build/pallas_call | solution.py:63
  21.9 2.4 %shard_map.114 = (bf16[256,512]{1,0:T(8,128)(2,1)S(1)}, bf16[256,512]{1,0:T(8,128)(2,1)S(1)}, bf16[128,512]{1,0:T(8,128)(2,1)S(1)}, bf16[128,512]{1,0:T(8,128)(2,1)S(1)}, bf16[256,512]{1,0:T(8,128)(2,1)S(1)}) custom-call(bf16[256,512]{1,0:T(8,128)(2,1)S(1)} %copy-done, bf16[256,512]{1,0:T(8,128)(2,1)S(1)} %collective-permute-done.refs_1_, ...), custom_call_target="tpu_custom_call" | custom-call | flops 2147483648 | bytes 8388608 | tf_op jit(solution)/shard_map/pallas_call | solution.py:161
  24.3 1.9 %collective-permute-start.7 = (bf16[256,512]{1,0:T(8,128)(2,1)S(1)}, bf16[256,512]{1,0:T(8,128)(2,1)S(1)}, u32[]{:S(2)}, u32[]{:S(2)}) collective-permute-start(bf16[256,512]{1,0:T(8,128)(2,1)S(1)} %get-tuple-element.28), channel_id=1, source_target_pairs={{0,4},{4,0},{8,12},{12,8},{16,20},{20,16},{24,28},{28,24},{1,5},{5... | collective-permute-start | bytes 786440 | tf_op jit(solution)/shard_map/ppermute | solution.py:23
  26.2 1.1 %collective-permute-start.4 = (bf16[256,512]{1,0:T(8,128)(2,1)S(1)}, bf16[256,512]{1,0:T(8,128)(2,1)S(1)}, u32[]{:S(2)}, u32[]{:S(2)}) collective-permute-start(bf16[256,512]{1,0:T(8,128)(2,1)S(1)} %get-tuple-element.24), channel_id=1, source_target_pairs={{0,8},{4,12},{8,0},{12,4},{16,24},{20,28},{24,16},{28,20},{1,9},{5... | collective-permute-start | bytes 786440 | tf_op jit(solution)/shard_map/ppermute | solution.py:23
  27.5 5.1 %collective-permute-done.17.refs_3_ = bf16[256,512]{1,0:T(8,128)(2,1)S(1)} collective-permute-done((bf16[256,512]{1,0:T(8,128)(2,1)S(1)}, bf16[256,512]{1,0:T(8,128)(2,1)S(1)}, u32[]{:S(2)}, u32[]{:S(2)}) %collective-permute-start.17) | collective-permute-done | bytes 262176 | tf_op jit(solution)/shard_map/ppermute | solution.py:23
  32.6 4.0 %backward_early.1 = (f32[256,512]{1,0:T(8,128)S(1)}, f32[256,512]{1,0:T(8,128)S(1)}, f32[256,512]{1,0:T(8,128)S(1)}, f32[256,512]{1,0:T(8,128)S(1)}) custom-call(bf16[256,512]{1,0:T(8,128)(2,1)S(1)} %copy-done.1, bf16[256,512]{1,0:T(8,128)(2,1)S(1)} %collective-permute-done.15.refs_1_, bf16[256,512]{1,0:T(8,128)(2,1)S(1)} %collective-permute-done.16.refs_2_, ...), custom_call_target="tpu_custom_call" | custom-call | flops 4294967296 | bytes 8388608 | tf_op jit(solution)/shard_map/backward_early/pallas_call | solution.py:115
  36.6 6.0 %collective-permute-done.14.refs_0_ = bf16[256,512]{1,0:T(8,128)(2,1)S(1)} collective-permute-done((bf16[256,512]{1,0:T(8,128)(2,1)S(1)}, bf16[256,512]{1,0:T(8,128)(2,1)S(1)}, u32[]{:S(2)}, u32[]{:S(2)}) %collective-permute-start.14) | collective-permute-done | bytes 262176 | tf_op jit(solution)/shard_map/ppermute | solution.py:23
  43.1 2.4 %shard_map.113 = (bf16[256,512]{1,0:T(8,128)(2,1)S(1)}, bf16[256,512]{1,0:T(8,128)(2,1)S(1)}, bf16[128,512]{1,0:T(8,128)(2,1)S(1)}, bf16[128,512]{1,0:T(8,128)(2...) custom-call(bf16[256,512]{1,0:T(8,128)(2,1)S(1)} %copy-done, ...), custom_call_target="tpu_custom_call" | custom-call | flops 2147483648 | bytes 8388608 | tf_op jit(solution)/shard_map/pallas_call | solution.py:161
  45.7 0.6 collective-permute-start.8
  46.2 1.5 %collective-permute-start.3 = (bf16[256,512]{1,0:T(8,128)(2,1)S(1)}, bf16[256,512]{1,0:T(8,128)(2,1)S(1)}, u32[]{:S(2)}, u32[]{:S(2)}) collective-permute-start(bf16[256,512]{1,0:T(8,128)(2,1)S(1)} %get-tuple-element.22), channel_id=1, source_target_pairs={{0,8},{4,12},{8,0},{12,4},{16,24},{20,28},{24,16},{28,20},{1,9},{5... | collective-permute-start | bytes 786440 | tf_op jit(solution)/shard_map/ppermute | solution.py:23
  47.8 1.5 %collective-permute-start.10 = (bf16[128,512]{1,0:T(8,128)(2,1)S(1)}, bf16[128,512]{1,0:T(8,128)(2,1)S(1)}, u32[]{:S(2)}, u32[]{:S(2)}) collective-permute-start(bf16[128,512]{1,0:T(8,128)(2,1)S(1)} %get-tuple-element.30), channel_id=1, source_target_pairs={{0,4},{4,0},{8,12},{12,8},{16,20},{20,16},{24,28},{28,24},{1,5},{5... | collective-permute-start | bytes 393224 | tf_op jit(solution)/shard_map/ppermute | solution.py:23
  49.3 0.5 collective-permute-start.6
  49.9 1.6 %collective-permute-start.5 = (bf16[256,512]{1,0:T(8,128)(2,1)S(1)}, bf16[256,512]{1,0:T(8,128)(2,1)S(1)}, u32[]{:S(2)}, u32[]{:S(2)}) collective-permute-start(bf16[256,512]{1,0:T(8,128)(2,1)S(1)} %join.4), channel_id=1, source_target_pairs={{0,4},{4,0},{8,12},{12,8},{16,20},{20,16},{24,28},{28,24},{1,5},{5... | collective-permute-start | bytes 786440 | tf_op jit(solution)/shard_map/ppermute | solution.py:23
  51.4 0.5 shard_map.117
  51.9 2.2 %collective-permute-done.10.refs_1_ = bf16[128,512]{1,0:T(8,128)(2,1)S(1)} collective-permute-done((bf16[128,512]{1,0:T(8,128)(2,1)S(1)}, bf16[128,512]{1,0:T(8,128)(2,1)S(1)}, u32[]{:S(2)}, u32[]{:S(2)}) %collective-permute-start.10) | collective-permute-done | bytes 131104 | tf_op jit(solution)/shard_map/ppermute | solution.py:23
  54.2 0.8 %collective-permute-done.8.refs_2_ = bf16[256,512]{1,0:T(8,128)(2,1)S(1)} collective-permute-done((bf16[256,512]{1,0:T(8,128)(2,1)S(1)}, bf16[256,512]{1,0:T(8,128)(2,1)S(1)}, u32[]{:S(2)}, u32[]{:S(2)}) %collective-permute-start.8) | collective-permute-done | bytes 262176 | tf_op jit(solution)/shard_map/ppermute | solution.py:23
  54.9 1.5 %collective-permute-start.21 = (bf16[256,512]{1,0:T(8,128)(2,1)S(1)}, bf16[256,512]{1,0:T(8,128)(2,1)S(1)}, u32[]{:S(2)}, u32[]{:S(2)}) collective-permute-start(bf16[256,512]{1,0:T(8,128)(2,1)S(1)} %get-tuple-element.39), channel_id=1, source_target_pairs={{0,2},{1,3},{2,0},{3,1},{4,6},{5,7},{6,4},{7,5},{8,10},{9,11},{10,... | collective-permute-start | bytes 786440 | tf_op jit(solution)/shard_map/ppermute | solution.py:23
  57.0 3.3 %collective-permute-start.11 = (bf16[128,512]{1,0:T(8,128)(2,1)S(1)}, bf16[128,512]{1,0:T(8,128)(2,1)S(1)}, u32[]{:S(2)}, u32[]{:S(2)}) collective-permute-start(bf16[128,512]{1,0:T(8,128)(2,1)S(1)} %join.7), channel_id=1, source_target_pairs={{0,16},{4,20},{8,24},{12,28},{16,0},{20,4},{24,8},{28,12},{1,17},{... | collective-permute-start | bytes 393224 | tf_op jit(solution)/shard_map/ppermute | solution.py:23
  60.3 3.5 %collective-permute-start.9 = (bf16[128,512]{1,0:T(8,128)(2,1)S(1)}, bf16[128,512]{1,0:T(8,128)(2,1)S(1)}, u32[]{:S(2)}, u32[]{:S(2)}) collective-permute-start(bf16[128,512]{1,0:T(8,128)(2,1)S(1)} %join.6), channel_id=1, source_target_pairs={{0,16},{4,20},{8,24},{12,28},{16,0},{20,4},{24,8},{28,12},{1,17},{... | collective-permute-start | bytes 393224 | tf_op jit(solution)/shard_map/ppermute | solution.py:23
  63.8 5.3 %collective-permute-done.11.refs_4_ = bf16[128,512]{1,0:T(8,128)(2,1)S(1)} collective-permute-done((bf16[128,512]{1,0:T(8,128)(2,1)S(1)}, bf16[128,512]{1,0:T(8,128)(2,1)S(1)}, u32[]{:S(2)}, u32[]{:S(2)}) %collective-permute-start.11) | collective-permute-done | bytes 131104 | tf_op jit(solution)/shard_map/ppermute | solution.py:23
  69.1 2.5 %collective-permute-done.9.refs_3_ = bf16[128,512]{1,0:T(8,128)(2,1)S(1)} collective-permute-done((bf16[128,512]{1,0:T(8,128)(2,1)S(1)}, bf16[128,512]{1,0:T(8,128)(2,1)S(1)}, u32[]{:S(2)}, u32[]{:S(2)}) %collective-permute-start.9) | collective-permute-done | bytes 131104 | tf_op jit(solution)/shard_map/ppermute | solution.py:23
  71.6 1.1 %shard_map.115 = bf16[256,512]{1,0:T(8,128)(2,1)} custom-call(bf16[256,512]{1,0:T(8,128)(2,1)S(1)} %get-tuple-element.21.refs_0_, bf16[256,512]{1,0:T(8,128)(2,1)S(1)} %collective-permute-done.3.refs_1_, bf16[256,512]{1,0:T(8,128)(2,1)S(1)} %collective-permute-done.5.refs_2_, bf16[128,512]{1,0:T(8,128)(2,1)S(1)} %collective-permute-done.9.refs_3_, ...), custom_call_target="tpu_custom_call" | custom-call | flops 1000000000 | bytes 2097152 | tf_op jit(solution)/shard_map/pallas_call | solution.py:227
  72.7 1.0 %shard_map.118 = bf16[256,512]{1,0:T(8,128)(2,1)} custom-call(bf16[256,512]{1,0:T(8,128)(2,1)S(1)} %get-tuple-element.37.refs_0_, bf16[256,512]{1,0:T(8,128)(2,1)S(1)} %collective-permute-done.20.refs_1_, bf16[256,512]{1,0:T(8,128)(2,1)S(1)} %collective-permute-done.21.refs_2_, bf16[256,256]{1,0:T(8,128)(2,1)S(1)} %copy-done.7, ...), custom_call_target="tpu_custom_call" | custom-call | flops 1000000000 | bytes 2097152 | tf_op jit(solution)/shard_map/pallas_call | solution.py:227
  (46 shorter events, 1.5 us)
Async XLA Ops:
  0.6 19.2 %slice-start = ((s8[5570560]{0:T(1024)(128)(4,1)}), s8[4194304]{0:T(1024)(128)(4,1)S(1)}, s32[]{:S(2)}) async-start(s8[5570560]{0:T(1024)(128)(4,1)} %bitcast.1), calls=%async_computation | async-start | bytes 8388608
  0.6 19.2 %copy-start.4 = (s32[1,1,170]{2,1,0:T(1,128)S(1)}, s32[1,1,170]{2,1,0:T(1,128)}, u32[]{:S(2)}) copy-start(s32[1,1,170]{2,1,0:T(1,128)} %rows.1) | copy-start | bytes 2044
  0.7 19.2 %copy-start.5 = (s32[1,1,170]{2,1,0:T(1,128)S(1)}, s32[1,1,170]{2,1,0:T(1,128)}, u32[]{:S(2)}) copy-start(s32[1,1,170]{2,1,0:T(1,128)} %cols.1) | copy-start | bytes 2044
  0.7 16.4 %collective-permute-start.12 = (bf16[256,512]{1,0:T(8,128)(2,1)}, bf16[256,512]{1,0:T(8,128)(2,1)S(1)}, u32[]{:S(2)}, u32[]{:S(2)}) collective-permute-start(bf16[256,512]{1,0:T(8,128)(2,1)} %refs_0_.5), channel_id=1, source_target_pairs={{0,16},{4,20},{8,24},{12,28},{16,0},{20,4},{24,8},{28,12},{1,17},{... | collective-permute-start | bytes 786440 | tf_op jit(solution)/shard_map/ppermute | solution.py:23
  4.8 13.0 %collective-permute-start.16 = (bf16[256,512]{1,0:T(8,128)(2,1)}, bf16[256,512]{1,0:T(8,128)(2,1)S(1)}, u32[]{:S(2)}, u32[]{:S(2)}) collective-permute-start(bf16[256,512]{1,0:T(8,128)(2,1)} %refs_0_.5), channel_id=1, source_target_pairs={{0,8},{4,12},{8,0},{12,4},{16,24},{20,28},{24,16},{28,20},{1,9},{5... | collective-permute-start | bytes 786440 | tf_op jit(solution)/shard_map/ppermute | solution.py:23
  6.4 19.8 %collective-permute-start.15 = (bf16[256,512]{1,0:T(8,128)(2,1)}, bf16[256,512]{1,0:T(8,128)(2,1)S(1)}, u32[]{:S(2)}, u32[]{:S(2)}) collective-permute-start(bf16[256,512]{1,0:T(8,128)(2,1)} %refs_0_.5), channel_id=1, source_target_pairs={{0,4},{4,0},{8,12},{12,8},{16,20},{20,16},{24,28},{28,24},{1,5},{5... | collective-permute-start | bytes 786440 | tf_op jit(solution)/shard_map/ppermute | solution.py:23
  7.9 11.4 %collective-permute-start.1 = (bf16[256,512]{1,0:T(8,128)(2,1)}, bf16[256,512]{1,0:T(8,128)(2,1)S(1)}, u32[]{:S(2)}, u32[]{:S(2)}) collective-permute-start(bf16[256,512]{1,0:T(8,128)(2,1)} %refs_4_.1), channel_id=1, source_target_pairs={{0,2},{1,3},{2,0},{3,1},{4,6},{5,7},{6,4},{7,5},{8,10},{9,11},{10,... | collective-permute-start | bytes 786440 | tf_op jit(solution)/shard_map/ppermute | solution.py:23
  9.4 10.4 %collective-permute-start = (bf16[256,512]{1,0:T(8,128)(2,1)}, bf16[256,512]{1,0:T(8,128)(2,1)S(1)}, u32[]{:S(2)}, u32[]{:S(2)}) collective-permute-start(bf16[256,512]{1,0:T(8,128)(2,1)} %refs_4_.1), channel_id=1, source_target_pairs={{0,1},{1,0},{2,3},{3,2},{4,5},{5,4},{6,7},{7,6},{8,9},{9,8},{10,11... | collective-permute-start | bytes 786440 | tf_op jit(solution)/shard_map/ppermute | solution.py:23
  10.0 9.8 %slice-start.1 = ((s8[5570560]{0:T(1024)(128)(4,1)}), s8[1376256]{0:T(1024)(128)(4,1)S(1)}, s32[]{:S(2)}) async-start(s8[5570560]{0:T(1024)(128)(4,1)} %bitcast.1), calls=%async_computation.1 | async-start | bytes 2752512
  17.0 10.3 %collective-permute-start.13 = (bf16[256,512]{1,0:T(8,128)(2,1)S(1)}, bf16[256,512]{1,0:T(8,128)(2,1)S(1)}, u32[]{:S(2)}, u32[]{:S(2)}) collective-permute-start(bf16[256,512]{1,0:T(8,128)(2,1)S(1)} %collective-permute-done.12.refs_4_), channel_id=1, source_target_pairs={{0,8},{4,12},{8,0},{12,4},{16,24},{20,28},{24,16},{28,20},{1,9},{5... | collective-permute-start | bytes 786440 | tf_op jit(solution)/shard_map/ppermute | solution.py:23
  17.8 9.7 %collective-permute-start.18 = (bf16[256,512]{1,0:T(8,128)(2,1)S(1)}, bf16[256,512]{1,0:T(8,128)(2,1)S(1)}, u32[]{:S(2)}, u32[]{:S(2)}) collective-permute-start(bf16[256,512]{1,0:T(8,128)(2,1)S(1)} %collective-permute-done.12.refs_4_), channel_id=1, source_target_pairs={{0,4},{4,0},{8,12},{12,8},{16,20},{20,16},{24,28},{28,24},{1,5},{5... | collective-permute-start | bytes 786440 | tf_op jit(solution)/shard_map/ppermute | solution.py:23
  19.3 13.3 %collective-permute-start.17 = (bf16[256,512]{1,0:T(8,128)(2,1)S(1)}, bf16[256,512]{1,0:T(8,128)(2,1)S(1)}, u32[]{:S(2)}, u32[]{:S(2)}) collective-permute-start(bf16[256,512]{1,0:T(8,128)(2,1)S(1)} %collective-permute-done.16.refs_2_), channel_id=1, source_target_pairs={{0,4},{4,0},{8,12},{12,8},{16,20},{20,16},{24,28},{28,24},{1,5},{5... | collective-permute-start | bytes 786440 | tf_op jit(solution)/shard_map/ppermute | solution.py:23
  19.8 2.0 %collective-permute-start.2 = (bf16[256,512]{1,0:T(8,128)(2,1)S(1)}, bf16[256,512]{1,0:T(8,128)(2,1)S(1)}, u32[]{:S(2)}, u32[]{:S(2)}) collective-permute-start(bf16[256,512]{1,0:T(8,128)(2,1)S(1)} %collective-permute-done.1.refs_2_), channel_id=1, source_target_pairs={{0,1},{1,0},{2,3},{3,2},{4,5},{5,4},{6,7},{7,6},{8,9},{9,8},{10,11... | collective-permute-start | bytes 786440 | tf_op jit(solution)/shard_map/ppermute | solution.py:23
  19.8 2.0 %copy-start = (bf16[256,512]{1,0:T(8,128)(2,1)S(1)}, bf16[256,512]{1,0:T(8,128)(2,1)}, u32[]{:S(2)}) copy-start(bf16[256,512]{1,0:T(8,128)(2,1)} %refs_4_.1) | copy-start | bytes 786436
  21.8 10.7 %copy-start.1 = (bf16[256,512]{1,0:T(8,128)(2,1)S(1)}, bf16[256,512]{1,0:T(8,128)(2,1)}, u32[]{:S(2)}) copy-start(bf16[256,512]{1,0:T(8,128)(2,1)} %refs_0_.5) | copy-start | bytes 786436
  24.3 21.3 %collective-permute-start.7 = (bf16[256,512]{1,0:T(8,128)(2,1)S(1)}, bf16[256,512]{1,0:T(8,128)(2,1)S(1)}, u32[]{:S(2)}, u32[]{:S(2)}) collective-permute-start(bf16[256,512]{1,0:T(8,128)(2,1)S(1)} %get-tuple-element.28), channel_id=1, source_target_pairs={{0,4},{4,0},{8,12},{12,8},{16,20},{20,16},{24,28},{28,24},{1,5},{5... | collective-permute-start | bytes 786440 | tf_op jit(solution)/shard_map/ppermute | solution.py:23
  26.2 16.9 %copy-start.2 = (bf16[128,512]{1,0:T(8,128)(2,1)S(1)}, bf16[128,512]{1,0:T(8,128)(2,1)}, u32[]{:S(2)}) copy-start(bf16[128,512]{1,0:T(8,128)(2,1)} %refs_6_.1) | copy-start | bytes 393220
  26.2 16.9 %copy-start.3 = (bf16[256,128]{1,0:T(8,128)(2,1)S(1)}, bf16[256,128]{1,0:T(8,128)(2,1)}, u32[]{:S(2)}) copy-start(bf16[256,128]{1,0:T(8,128)(2,1)} %refs_5_.3) | copy-start | bytes 196612
  26.2 23.1 %collective-permute-start.4 = (bf16[256,512]{1,0:T(8,128)(2,1)S(1)}, bf16[256,512]{1,0:T(8,128)(2,1)S(1)}, u32[]{:S(2)}, u32[]{:S(2)}) collective-permute-start(bf16[256,512]{1,0:T(8,128)(2,1)S(1)} %get-tuple-element.24), channel_id=1, source_target_pairs={{0,8},{4,12},{8,0},{12,4},{16,24},{20,28},{24,16},{28,20},{1,9},{5... | collective-permute-start | bytes 786440 | tf_op jit(solution)/shard_map/ppermute | solution.py:23
  27.3 15.2 %collective-permute-start.14 = (bf16[256,512]{1,0:T(8,128)(2,1)S(1)}, bf16[256,512]{1,0:T(8,128)(2,1)S(1)}, u32[]{:S(2)}, u32[]{:S(2)}) collective-permute-start(bf16[256,512]{1,0:T(8,128)(2,1)S(1)} %collective-permute-done.13.refs_6_), channel_id=1, source_target_pairs={{0,4},{4,0},{8,12},{12,8},{16,20},{20,16},{24,28},{28,24},{1,5},{5... | collective-permute-start | bytes 786440 | tf_op jit(solution)/shard_map/ppermute | solution.py:23
  43.0 28.6 %copy-start.7 = (bf16[256,256]{1,0:T(8,128)(2,1)S(1)}, bf16[256,256]{1,0:T(8,128)(2,1)}, u32[]{:S(2)}) copy-start(bf16[256,256]{1,0:T(8,128)(2,1)} %refs_3_.1) | copy-start | bytes 393220
  43.0 6.8 %collective-permute-start.19 = (bf16[256,512]{1,0:T(8,128)(2,1)S(1)}, bf16[256,512]{1,0:T(8,128)(2,1)S(1)}, u32[]{:S(2)}, u32[]{:S(2)}) collective-permute-start(bf16[256,512]{1,0:T(8,128)(2,1)S(1)} %get-tuple-element.36), channel_id=1, source_target_pairs={{0,1},{1,0},{2,3},{3,2},{4,5},{5,4},{6,7},{7,6},{8,9},{9,8},{10,11... | collective-permute-start | bytes 786440 | tf_op jit(solution)/shard_map/ppermute | solution.py:23
  45.6 27.1 %copy-start.6 = (bf16[256,512]{1,0:T(8,128)(2,1)S(1)}, bf16[256,512]{1,0:T(8,128)(2,1)}, u32[]{:S(2)}) copy-start(bf16[256,512]{1,0:T(8,128)(2,1)} %refs_5_.5) | copy-start | bytes 786436
  45.7 9.2 %collective-permute-start.8 = (bf16[256,512]{1,0:T(8,128)(2,1)S(1)}, bf16[256,512]{1,0:T(8,128)(2,1)S(1)}, u32[]{:S(2)}, u32[]{:S(2)}) collective-permute-start(bf16[256,512]{1,0:T(8,128)(2,1)S(1)} %join.5), channel_id=1, source_target_pairs={{0,8},{4,12},{8,0},{12,4},{16,24},{20,28},{24,16},{28,20},{1,9},{5... | collective-permute-start | bytes 786440 | tf_op jit(solution)/shard_map/ppermute | solution.py:23
  46.2 14.0 %collective-permute-start.3 = (bf16[256,512]{1,0:T(8,128)(2,1)S(1)}, bf16[256,512]{1,0:T(8,128)(2,1)S(1)}, u32[]{:S(2)}, u32[]{:S(2)}) collective-permute-start(bf16[256,512]{1,0:T(8,128)(2,1)S(1)} %get-tuple-element.22), channel_id=1, source_target_pairs={{0,8},{4,12},{8,0},{12,4},{16,24},{20,28},{24,16},{28,20},{1,9},{5... | collective-permute-start | bytes 786440 | tf_op jit(solution)/shard_map/ppermute | solution.py:23
  47.8 6.4 %collective-permute-start.10 = (bf16[128,512]{1,0:T(8,128)(2,1)S(1)}, bf16[128,512]{1,0:T(8,128)(2,1)S(1)}, u32[]{:S(2)}, u32[]{:S(2)}) collective-permute-start(bf16[128,512]{1,0:T(8,128)(2,1)S(1)} %get-tuple-element.30), channel_id=1, source_target_pairs={{0,4},{4,0},{8,12},{12,8},{16,20},{20,16},{24,28},{28,24},{1,5},{5... | collective-permute-start | bytes 393224 | tf_op jit(solution)/shard_map/ppermute | solution.py:23
  49.3 7.7 %collective-permute-start.6 = (bf16[128,512]{1,0:T(8,128)(2,1)S(1)}, bf16[128,512]{1,0:T(8,128)(2,1)S(1)}, u32[]{:S(2)}, u32[]{:S(2)}) collective-permute-start(bf16[128,512]{1,0:T(8,128)(2,1)S(1)} %get-tuple-element.26), channel_id=1, source_target_pairs={{0,4},{4,0},{8,12},{12,8},{16,20},{20,16},{24,28},{28,24},{1,5},{5... | collective-permute-start | bytes 393224 | tf_op jit(solution)/shard_map/ppermute | solution.py:23
  49.9 13.9 %collective-permute-start.5 = (bf16[256,512]{1,0:T(8,128)(2,1)S(1)}, bf16[256,512]{1,0:T(8,128)(2,1)S(1)}, u32[]{:S(2)}, u32[]{:S(2)}) collective-permute-start(bf16[256,512]{1,0:T(8,128)(2,1)S(1)} %join.4), channel_id=1, source_target_pairs={{0,4},{4,0},{8,12},{12,8},{16,20},{20,16},{24,28},{28,24},{1,5},{5... | collective-permute-start | bytes 786440 | tf_op jit(solution)/shard_map/ppermute | solution.py:23
  54.2 18.5 %collective-permute-start.20 = (bf16[256,512]{1,0:T(8,128)(2,1)S(1)}, bf16[256,512]{1,0:T(8,128)(2,1)S(1)}, u32[]{:S(2)}, u32[]{:S(2)}) collective-permute-start(bf16[256,512]{1,0:T(8,128)(2,1)S(1)} %get-tuple-element.38), channel_id=1, source_target_pairs={{0,1},{1,0},{2,3},{3,2},{4,5},{5,4},{6,7},{7,6},{8,9},{9,8},{10,11... | collective-permute-start | bytes 786440 | tf_op jit(solution)/shard_map/ppermute | solution.py:23
  54.9 17.7 %collective-permute-start.21 = (bf16[256,512]{1,0:T(8,128)(2,1)S(1)}, bf16[256,512]{1,0:T(8,128)(2,1)S(1)}, u32[]{:S(2)}, u32[]{:S(2)}) collective-permute-start(bf16[256,512]{1,0:T(8,128)(2,1)S(1)} %get-tuple-element.39), channel_id=1, source_target_pairs={{0,2},{1,3},{2,0},{3,1},{4,6},{5,7},{6,4},{7,5},{8,10},{9,11},{10,... | collective-permute-start | bytes 786440 | tf_op jit(solution)/shard_map/ppermute | solution.py:23
  57.0 12.1 %collective-permute-start.11 = (bf16[128,512]{1,0:T(8,128)(2,1)S(1)}, bf16[128,512]{1,0:T(8,128)(2,1)S(1)}, u32[]{:S(2)}, u32[]{:S(2)}) collective-permute-start(bf16[128,512]{1,0:T(8,128)(2,1)S(1)} %join.7), channel_id=1, source_target_pairs={{0,16},{4,20},{8,24},{12,28},{16,0},{20,4},{24,8},{28,12},{1,17},{... | collective-permute-start | bytes 393224 | tf_op jit(solution)/shard_map/ppermute | solution.py:23
  60.3 11.3 %collective-permute-start.9 = (bf16[128,512]{1,0:T(8,128)(2,1)S(1)}, bf16[128,512]{1,0:T(8,128)(2,1)S(1)}, u32[]{:S(2)}, u32[]{:S(2)}) collective-permute-start(bf16[128,512]{1,0:T(8,128)(2,1)S(1)} %join.6), channel_id=1, source_target_pairs={{0,16},{4,20},{8,24},{12,28},{16,0},{20,4},{24,8},{28,12},{1,17},{... | collective-permute-start | bytes 393224 | tf_op jit(solution)/shard_map/ppermute | solution.py:23
where the time goes:
time: 73.9 us; the launch traced here: 73.7 us
  starting transfers between devices  28.8 us (39%)
  waiting for transfers between devices  28.1 us (38%)
  Pallas kernels  15.3 us (21%)
  between operations  1.53 us (2%)
    ppermute x22, starting transfers between devices, swap(): return lax.ppermute(value, axis, [(i, i ^ mask) for i in range(size)])  28.8 us
    ppermute x22, waiting for transfers between devices, swap(): return lax.ppermute(value, axis, [(i, i ^ mask) for i in range(size)])  28.1 us
    pallas_call x2, Pallas kernels, forward(): pl.pallas_call(functools.partial(forward_kernel, parts, len(picks), cuts)...  4.84 us
    pallas_call x1, Pallas kernels, early(): pl.pallas_call(functools.partial(early_kernel, parts), in_specs=[in_vmem(...  3.99 us
    pallas_call x2, Pallas kernels, finish(): pl.pallas_call(functools.partial(kernel, len(terms), len(halves)), in_spe...  2.08 us
    pallas_call x1, Pallas kernels, build(): pl.pallas_call(functools.partial(build_kernel, per_chunk), in_specs=[smem...  1.97 us
  transfers between devices with their start and end apart: 22, of which 8 were waited for; matrix products, arithmetic and copies ran while one was open for 0% of the time, Pallas kernels for 19%

commit v1 on v0

--- a/solution.py
+++ b/solution.py
@@ -174,25 +174,14 @@
     return groups, outs
 
 
-def join_kernel(start, *refs):
-    *terms, out = refs
-    height = out.shape[0]
-    total = None
-    for ref in terms:
-        value = ref[...] if ref.shape[0] == height else ref[start : start + height, :]
-        value = value.astype(F32)
-        total = value if total is None else total + value
-    out[...] = total.astype(BF16)
-
-
-def join(terms, start=0):
-    return join_call(terms, start)
-
-
-def join_call(terms, start):
-    return pl.pallas_call(
-        functools.partial(join_kernel, start),
-        in_specs=[in_vmem()] * len(terms),
+def join_kernel(first, second, out):
+    out[...] = (first[...].astype(F32) + second[...].astype(F32)).astype(BF16)
+
+
+def join(terms):
+    return pl.pallas_call(
+        join_kernel,
+        in_specs=[in_vmem()] * 2,
         out_specs=in_vmem(),
         out_shape=jax.ShapeDtypeStruct(terms[0].shape, BF16),
         compiler_params=pltpu.CompilerParams(vmem_limit_bytes=4 * 2**20),
@@ -236,7 +225,7 @@
 
 def per_device(state, adjoint, features, cotangent, mixing, input_weight, tiles, tile_rows, tile_cols, live_tiles):
     n_row, n_col = lax.axis_size("row"), lax.axis_size("col")
-    hidden, nodes = state.shape
+    _, nodes = state.shape
     slab = tiles[0, 0]
     side = slab.shape[-1]
     half_row, half_col = n_row // 2, n_col // 2
@@ -270,16 +259,14 @@
     mine, (base,) = forward(states, dense, (input_weight, features), cuts)
     corner = join((others[0][0], direct))
     flows = [mine[0][0], by_row(mine[1][0], 2), by_row(corner, 1)]
-    halves, relayed = [], None
+    halves = []
     for k in reversed(range(2, half_row)):
         if k % 2:
-            relayed = by_row(join((mine[k][0], crossed[k][0])), 2)
+            flows.append(by_row(join((mine[k][0], crossed[k][0])), 2 * k))
             continue
-        last = () if relayed is None else (relayed,)
         for i in range(2):
-            pair = join((mine[k][i], crossed[k][i], *last), i * hidden // 2)
+            pair = join((mine[k][i], crossed[k][i]))
             halves.append(by_row(pair, 2 * k))
-        relayed = None
     new_state = finish(state_kernel, flows, halves, (mixing, base))
 
     sums = early(adjoints[:-1], dense, n_col)

time: 73.9 us -> 79.3 us (1.073)
  waiting for transfers between devices: 28.1 us -> 36 us
  starting transfers between devices: 28.8 us -> 26.3 us
    ppermute x22, waiting for transfers between devices: 28.1 us -> 36 us  [swap(): return lax.ppermute(value, axis, [(i, i ^ mask) for i in range(size)])]
    ppermute x22, starting transfers between devices: 28.8 us -> 26.3 us  [swap(): return lax.ppermute(value, axis, [(i, i ^ mask) for i in range(size)])]
  transfers between devices with their start and end apart: 22 -> 22, of which waited for: 8 -> 5; matrix products, arithmetic and copies ran while one was open for 0% -> 0% of each run, Pallas kernels for 19% -> 18%
where the time goes in v1:
time: 79.3 us; the launch traced here: 79.1 us
  waiting for transfers between devices  36 us (45%)
  starting transfers between devices  26.3 us (33%)
  Pallas kernels  15.3 us (19%)
  between operations  1.56 us (2%)
    ppermute x22, waiting for transfers between devices, swap(): return lax.ppermute(value, axis, [(i, i ^ mask) for i in range(size)])  36 us
    ppermute x22, starting transfers between devices, swap(): return lax.ppermute(value, axis, [(i, i ^ mask) for i in range(size)])  26.3 us
    pallas_call x2, Pallas kernels, forward(): pl.pallas_call(functools.partial(forward_kernel, parts, len(picks), cuts)...  4.84 us
    pallas_call x1, Pallas kernels, early(): pl.pallas_call(functools.partial(early_kernel, parts), in_specs=[in_vmem(...  3.99 us
    pallas_call x2, Pallas kernels, finish(): pl.pallas_call(functools.partial(kernel, len(terms), len(halves)), in_spe...  2.1 us
    pallas_call x1, Pallas kernels, build(): pl.pallas_call(functools.partial(build_kernel, per_chunk), in_specs=[smem...  1.97 us
  transfers between devices with their start and end apart: 22, of which 5 were waited for; matrix products, arithmetic and copies ran while one was open for 0% of the time, Pallas kernels for 18%

profile of v1, /device:TPU:0, one launch (start us, length us, event | category | flops | bytes accessed | tf_op | source)
XLA Modules:
  0.0 79.1 jit_solution(11481961769423809472)
XLA Ops:
  0.7 4.1 %collective-permute-start.12 = (bf16[256,512]{1,0:T(8,128)(2,1)}, bf16[256,512]{1,0:T(8,128)(2,1)S(1)}, u32[]{:S(2)}, u32[]{:S(2)}) collective-permute-start(bf16[256,512]{1,0:T(8,128)(2,1)} %refs_0_.5), channel_id=1, source_target_pairs={{0,16},{4,20},{8,24},{12,28},{16,0},{20,4},{24,8},{28,12},{1,17},{... | collective-permute-start | bytes 786440 | tf_op jit(solution)/shard_map/ppermute | solution.py:23
  4.8 1.6 %collective-permute-start.16 = (bf16[256,512]{1,0:T(8,128)(2,1)}, bf16[256,512]{1,0:T(8,128)(2,1)S(1)}, u32[]{:S(2)}, u32[]{:S(2)}) collective-permute-start(bf16[256,512]{1,0:T(8,128)(2,1)} %refs_0_.5), channel_id=1, source_target_pairs={{0,8},{4,12},{8,0},{12,4},{16,24},{20,28},{24,16},{28,20},{1,9},{5... | collective-permute-start | bytes 786440 | tf_op jit(solution)/shard_map/ppermute | solution.py:23
  6.4 1.5 %collective-permute-start.15 = (bf16[256,512]{1,0:T(8,128)(2,1)}, bf16[256,512]{1,0:T(8,128)(2,1)S(1)}, u32[]{:S(2)}, u32[]{:S(2)}) collective-permute-start(bf16[256,512]{1,0:T(8,128)(2,1)} %refs_0_.5), channel_id=1, source_target_pairs={{0,4},{4,0},{8,12},{12,8},{16,20},{20,16},{24,28},{28,24},{1,5},{5... | collective-permute-start | bytes 786440 | tf_op jit(solution)/shard_map/ppermute | solution.py:23
  7.9 1.5 %collective-permute-start.1 = (bf16[256,512]{1,0:T(8,128)(2,1)}, bf16[256,512]{1,0:T(8,128)(2,1)S(1)}, u32[]{:S(2)}, u32[]{:S(2)}) collective-permute-start(bf16[256,512]{1,0:T(8,128)(2,1)} %refs_4_.1), channel_id=1, source_target_pairs={{0,2},{1,3},{2,0},{3,1},{4,6},{5,7},{6,4},{7,5},{8,10},{9,11},{10,... | collective-permute-start | bytes 786440 | tf_op jit(solution)/shard_map/ppermute | solution.py:23
  10.0 1.2 %clear.1.blank = bf16[2048,4096]{1,0:T(8,128)(2,1)S(1)} custom-call(), custom_call_target="tpu_custom_call" | custom-call | flops 5000000000 | bytes 16777216 | tf_op jit(solution)/shard_map/clear/pallas_call | solution.py:37
  11.3 5.8 %collective-permute-done.12.refs_4_ = bf16[256,512]{1,0:T(8,128)(2,1)S(1)} collective-permute-done((bf16[256,512]{1,0:T(8,128)(2,1)}, bf16[256,512]{1,0:T(8,128)(2,1)S(1)}, u32[]{:S(2)}, u32[]{:S(2)}) %collective-permute-start.12) | collective-permute-done | bytes 262176 | tf_op jit(solution)/shard_map/ppermute | solution.py:23
  17.0 0.7 collective-permute-start.13
  17.8 1.5 %collective-permute-start.18 = (bf16[256,512]{1,0:T(8,128)(2,1)S(1)}, bf16[256,512]{1,0:T(8,128)(2,1)S(1)}, u32[]{:S(2)}, u32[]{:S(2)}) collective-permute-start(bf16[256,512]{1,0:T(8,128)(2,1)S(1)} %collective-permute-done.12.refs_4_), channel_id=1, source_target_pairs={{0,4},{4,0},{8,12},{12,8},{16,20},{20,16},{24,28},{28,24},{1,5},{5... | collective-permute-start | bytes 786440 | tf_op jit(solution)/shard_map/ppermute | solution.py:23
  19.3 0.5 collective-permute-start.17
  19.8 2.0 %build.1.refs_4_.refs_7_.refs_1_ = bf16[2048,4096]{1,0:T(8,128)(2,1)S(1)} custom-call(s32[1,1,170]{2,1,0:T(1,128)S(1)} %copy-done.4, s32[1,1,170]{2,1,0:T(1,128)S(1)} %copy-done.5, s32[1,1]{1,0:T(1,128)S(6)} %copy.14.count, bf16[170,128,128]{2,1,0:T(8,128)(2,1)S(1)} %bitcast.3, bf16[2048,4096]{1,0:T(8,128)(2,1)S(1)} %clear.1.blank), custom_call_target="tpu_custom_call", output_to_operand_aliasing={{}: (4, {})} | custom-call | flops 5000000000 | bytes 5570560 | tf_op jit(solution)/shard_map/build/pallas_call | solution.py:63
  21.9 2.4 %shard_map.114 = (bf16[256,512]{1,0:T(8,128)(2,1)S(1)}, bf16[256,512]{1,0:T(8,128)(2,1)S(1)}, bf16[128,512]{1,0:T(8,128)(2,1)S(1)}, bf16[128,512]{1,0:T(8,128)(2,1)S(1)}, bf16[256,512]{1,0:T(8,128)(2,1)S(1)}) custom-call(bf16[256,512]{1,0:T(8,128)(2,1)S(1)} %copy-done, bf16[256,512]{1,0:T(8,128)(2,1)S(1)} %collective-permute-done.refs_1_, ...), custom_call_target="tpu_custom_call" | custom-call | flops 2147483648 | bytes 8388608 | tf_op jit(solution)/shard_map/pallas_call | solution.py:161
  24.3 1.9 %collective-permute-start.10 = (bf16[128,512]{1,0:T(8,128)(2,1)S(1)}, bf16[128,512]{1,0:T(8,128)(2,1)S(1)}, u32[]{:S(2)}, u32[]{:S(2)}) collective-permute-start(bf16[128,512]{1,0:T(8,128)(2,1)S(1)} %get-tuple-element.30), channel_id=1, source_target_pairs={{0,4},{4,0},{8,12},{12,8},{16,20},{20,16},{24,28},{28,24},{1,5},{5... | collective-permute-start | bytes 393224 | tf_op jit(solution)/shard_map/ppermute | solution.py:23
  26.2 0.1 collective-permute-start.6
  26.4 1.1 %collective-permute-start.4 = (bf16[256,512]{1,0:T(8,128)(2,1)S(1)}, bf16[256,512]{1,0:T(8,128)(2,1)S(1)}, u32[]{:S(2)}, u32[]{:S(2)}) collective-permute-start(bf16[256,512]{1,0:T(8,128)(2,1)S(1)} %get-tuple-element.24), channel_id=1, source_target_pairs={{0,8},{4,12},{8,0},{12,4},{16,24},{20,28},{24,16},{28,20},{1,9},{5... | collective-permute-start | bytes 786440 | tf_op jit(solution)/shard_map/ppermute | solution.py:23
  27.5 1.9 %collective-permute-start.14 = (bf16[256,512]{1,0:T(8,128)(2,1)S(1)}, bf16[256,512]{1,0:T(8,128)(2,1)S(1)}, u32[]{:S(2)}, u32[]{:S(2)}) collective-permute-start(bf16[256,512]{1,0:T(8,128)(2,1)S(1)} %collective-permute-done.13.refs_6_), channel_id=1, source_target_pairs={{0,4},{4,0},{8,12},{12,8},{16,20},{20,16},{24,28},{28,24},{1,5},{5... | collective-permute-start | bytes 786440 | tf_op jit(solution)/shard_map/ppermute | solution.py:23
  29.4 3.2 %collective-permute-done.17.refs_3_ = bf16[256,512]{1,0:T(8,128)(2,1)S(1)} collective-permute-done((bf16[256,512]{1,0:T(8,128)(2,1)S(1)}, bf16[256,512]{1,0:T(8,128)(2,1)S(1)}, u32[]{:S(2)}, u32[]{:S(2)}) %collective-permute-start.17) | collective-permute-done | bytes 262176 | tf_op jit(solution)/shard_map/ppermute | solution.py:23
  32.6 4.0 %backward_early.1 = (f32[256,512]{1,0:T(8,128)S(1)}, f32[256,512]{1,0:T(8,128)S(1)}, f32[256,512]{1,0:T(8,128)S(1)}, f32[256,512]{1,0:T(8,128)S(1)}) custom-call(bf16[256,512]{1,0:T(8,128)(2,1)S(1)} %copy-done.1, bf16[256,512]{1,0:T(8,128)(2,1)S(1)} %collective-permute-done.15.refs_1_, bf16[256,512]{1,0:T(8,128)(2,1)S(1)} %collective-permute-done.16.refs_2_, ...), custom_call_target="tpu_custom_call" | custom-call | flops 4294967296 | bytes 8388608 | tf_op jit(solution)/shard_map/backward_early/pallas_call | solution.py:115
  36.6 8.8 %collective-permute-done.14.refs_0_ = bf16[256,512]{1,0:T(8,128)(2,1)S(1)} collective-permute-done((bf16[256,512]{1,0:T(8,128)(2,1)S(1)}, bf16[256,512]{1,0:T(8,128)(2,1)S(1)}, u32[]{:S(2)}, u32[]{:S(2)}) %collective-permute-start.14) | collective-permute-done | bytes 262176 | tf_op jit(solution)/shard_map/ppermute | solution.py:23
  45.4 0.5 shard_map.116
  46.0 2.4 %shard_map.113 = (bf16[256,512]{1,0:T(8,128)(2,1)S(1)}, bf16[256,512]{1,0:T(8,128)(2,1)S(1)}, bf16[128,512]{1,0:T(8,128)(2,1)S(1)}, bf16[128,512]{1,0:T(8,128)(2...) custom-call(bf16[256,512]{1,0:T(8,128)(2,1)S(1)} %copy-done, ...), custom_call_target="tpu_custom_call" | custom-call | flops 2147483648 | bytes 8388608 | tf_op jit(solution)/shard_map/pallas_call | solution.py:161
  48.4 0.6 collective-permute-start.3
  49.0 1.3 %collective-permute-start.8 = (bf16[128,512]{1,0:T(8,128)(2,1)S(1)}, bf16[128,512]{1,0:T(8,128)(2,1)S(1)}, u32[]{:S(2)}, u32[]{:S(2)}) collective-permute-start(bf16[128,512]{1,0:T(8,128)(2,1)S(1)} %get-tuple-element.28), channel_id=1, source_target_pairs={{0,4},{4,0},{8,12},{12,8},{16,20},{20,16},{24,28},{28,24},{1,5},{5... | collective-permute-start | bytes 393224 | tf_op jit(solution)/shard_map/ppermute | solution.py:23
  50.3 3.3 %collective-permute-start.11 = (bf16[128,512]{1,0:T(8,128)(2,1)S(1)}, bf16[128,512]{1,0:T(8,128)(2,1)S(1)}, u32[]{:S(2)}, u32[]{:S(2)}) collective-permute-start(bf16[128,512]{1,0:T(8,128)(2,1)S(1)} %join.7), channel_id=1, source_target_pairs={{0,16},{4,20},{8,24},{12,28},{16,0},{20,4},{24,8},{28,12},{1,17},{... | collective-permute-start | bytes 393224 | tf_op jit(solution)/shard_map/ppermute | solution.py:23
  53.7 1.3 %collective-permute-start.7 = (bf16[256,512]{1,0:T(8,128)(2,1)S(1)}, bf16[256,512]{1,0:T(8,128)(2,1)S(1)}, u32[]{:S(2)}, u32[]{:S(2)}) collective-permute-start(bf16[256,512]{1,0:T(8,128)(2,1)S(1)} %join.5), channel_id=1, source_target_pairs={{0,24},{4,28},{8,16},{12,20},{16,8},{20,12},{24,0},{28,4},{1,25},{... | collective-permute-start | bytes 786440 | tf_op jit(solution)/shard_map/ppermute | solution.py:23
  55.1 0.6 collective-permute-start.5
  55.7 0.5 shard_map.117
  56.2 3.7 %collective-permute-done.3.refs_1_ = bf16[256,512]{1,0:T(8,128)(2,1)S(1)} collective-permute-done((bf16[256,512]{1,0:T(8,128)(2,1)S(1)}, bf16[256,512]{1,0:T(8,128)(2,1)S(1)}, u32[]{:S(2)}, u32[]{:S(2)}) %collective-permute-start.3) | collective-permute-done | bytes 262176 | tf_op jit(solution)/shard_map/ppermute | solution.py:23
  60.0 1.5 %collective-permute-start.21 = (bf16[256,512]{1,0:T(8,128)(2,1)S(1)}, bf16[256,512]{1,0:T(8,128)(2,1)S(1)}, u32[]{:S(2)}, u32[]{:S(2)}) collective-permute-start(bf16[256,512]{1,0:T(8,128)(2,1)S(1)} %get-tuple-element.39), channel_id=1, source_target_pairs={{0,2},{1,3},{2,0},{3,1},{4,6},{5,7},{6,4},{7,5},{8,10},{9,11},{10,... | collective-permute-start | bytes 786440 | tf_op jit(solution)/shard_map/ppermute | solution.py:23
  61.5 1.0 %collective-permute-start.9 = (bf16[128,512]{1,0:T(8,128)(2,1)S(1)}, bf16[128,512]{1,0:T(8,128)(2,1)S(1)}, u32[]{:S(2)}, u32[]{:S(2)}) collective-permute-start(bf16[128,512]{1,0:T(8,128)(2,1)S(1)} %join.6), channel_id=1, source_target_pairs={{0,16},{4,20},{8,24},{12,28},{16,0},{20,4},{24,8},{28,12},{1,17},{... | collective-permute-start | bytes 393224 | tf_op jit(solution)/shard_map/ppermute | solution.py:23
  62.6 14.4 %collective-permute-done.9.refs_4_ = bf16[128,512]{1,0:T(8,128)(2,1)S(1)} collective-permute-done((bf16[128,512]{1,0:T(8,128)(2,1)S(1)}, bf16[128,512]{1,0:T(8,128)(2,1)S(1)}, u32[]{:S(2)}, u32[]{:S(2)}) %collective-permute-start.9) | collective-permute-done | bytes 131104 | tf_op jit(solution)/shard_map/ppermute | solution.py:23
  77.0 1.1 %shard_map.115 = bf16[256,512]{1,0:T(8,128)(2,1)} custom-call(bf16[256,512]{1,0:T(8,128)(2,1)S(1)} %get-tuple-element.21.refs_0_, bf16[256,512]{1,0:T(8,128)(2,1)S(1)} %collective-permute-done.3.refs_1_, bf16[256,512]{1,0:T(8,128)(2,1)S(1)} %collective-permute-done.5.refs_2_, bf16[256,512]{1,0:T(8,128)(2,1)S(1)} %collective-permute-done.7.refs_3_, ...), custom_call_target="tpu_custom_call" | custom-call | flops 1000000000 | bytes 2097152 | tf_op jit(solution)/shard_map/pallas_call | solution.py:216
  78.1 1.0 %shard_map.118 = bf16[256,512]{1,0:T(8,128)(2,1)} custom-call(bf16[256,512]{1,0:T(8,128)(2,1)S(1)} %get-tuple-element.37.refs_0_, bf16[256,512]{1,0:T(8,128)(2,1)S(1)} %collective-permute-done.20.refs_1_, bf16[256,512]{1,0:T(8,128)(2,1)S(1)} %collective-permute-done.21.refs_2_, bf16[256,256]{1,0:T(8,128)(2,1)S(1)} %copy-done.7, ...), custom_call_target="tpu_custom_call" | custom-call | flops 1000000000 | bytes 2097152 | tf_op jit(solution)/shard_map/pallas_call | solution.py:216
  (46 shorter events, 0.4 us)
Async XLA Ops:
  0.6 19.2 %slice-start = ((s8[5570560]{0:T(1024)(128)(4,1)}), s8[4194304]{0:T(1024)(128)(4,1)S(1)}, s32[]{:S(2)}) async-start(s8[5570560]{0:T(1024)(128)(4,1)} %bitcast.1), calls=%async_computation | async-start | bytes 8388608
  0.6 19.2 %copy-start.4 = (s32[1,1,170]{2,1,0:T(1,128)S(1)}, s32[1,1,170]{2,1,0:T(1,128)}, u32[]{:S(2)}) copy-start(s32[1,1,170]{2,1,0:T(1,128)} %rows.1) | copy-start | bytes 2044
  0.7 19.2 %copy-start.5 = (s32[1,1,170]{2,1,0:T(1,128)S(1)}, s32[1,1,170]{2,1,0:T(1,128)}, u32[]{:S(2)}) copy-start(s32[1,1,170]{2,1,0:T(1,128)} %cols.1) | copy-start | bytes 2044
  0.7 16.4 %collective-permute-start.12 = (bf16[256,512]{1,0:T(8,128)(2,1)}, bf16[256,512]{1,0:T(8,128)(2,1)S(1)}, u32[]{:S(2)}, u32[]{:S(2)}) collective-permute-start(bf16[256,512]{1,0:T(8,128)(2,1)} %refs_0_.5), channel_id=1, source_target_pairs={{0,16},{4,20},{8,24},{12,28},{16,0},{20,4},{24,8},{28,12},{1,17},{... | collective-permute-start | bytes 786440 | tf_op jit(solution)/shard_map/ppermute | solution.py:23
  4.8 13.0 %collective-permute-start.16 = (bf16[256,512]{1,0:T(8,128)(2,1)}, bf16[256,512]{1,0:T(8,128)(2,1)S(1)}, u32[]{:S(2)}, u32[]{:S(2)}) collective-permute-start(bf16[256,512]{1,0:T(8,128)(2,1)} %refs_0_.5), channel_id=1, source_target_pairs={{0,8},{4,12},{8,0},{12,4},{16,24},{20,28},{24,16},{28,20},{1,9},{5... | collective-permute-start | bytes 786440 | tf_op jit(solution)/shard_map/ppermute | solution.py:23
  6.4 19.8 %collective-permute-start.15 = (bf16[256,512]{1,0:T(8,128)(2,1)}, bf16[256,512]{1,0:T(8,128)(2,1)S(1)}, u32[]{:S(2)}, u32[]{:S(2)}) collective-permute-start(bf16[256,512]{1,0:T(8,128)(2,1)} %refs_0_.5), channel_id=1, source_target_pairs={{0,4},{4,0},{8,12},{12,8},{16,20},{20,16},{24,28},{28,24},{1,5},{5... | collective-permute-start | bytes 786440 | tf_op jit(solution)/shard_map/ppermute | solution.py:23
  7.9 11.4 %collective-permute-start.1 = (bf16[256,512]{1,0:T(8,128)(2,1)}, bf16[256,512]{1,0:T(8,128)(2,1)S(1)}, u32[]{:S(2)}, u32[]{:S(2)}) collective-permute-start(bf16[256,512]{1,0:T(8,128)(2,1)} %refs_4_.1), channel_id=1, source_target_pairs={{0,2},{1,3},{2,0},{3,1},{4,6},{5,7},{6,4},{7,5},{8,10},{9,11},{10,... | collective-permute-start | bytes 786440 | tf_op jit(solution)/shard_map/ppermute | solution.py:23
  9.4 10.4 %collective-permute-start = (bf16[256,512]{1,0:T(8,128)(2,1)}, bf16[256,512]{1,0:T(8,128)(2,1)S(1)}, u32[]{:S(2)}, u32[]{:S(2)}) collective-permute-start(bf16[256,512]{1,0:T(8,128)(2,1)} %refs_4_.1), channel_id=1, source_target_pairs={{0,1},{1,0},{2,3},{3,2},{4,5},{5,4},{6,7},{7,6},{8,9},{9,8},{10,11... | collective-permute-start | bytes 786440 | tf_op jit(solution)/shard_map/ppermute | solution.py:23
  10.0 9.8 %slice-start.1 = ((s8[5570560]{0:T(1024)(128)(4,1)}), s8[1376256]{0:T(1024)(128)(4,1)S(1)}, s32[]{:S(2)}) async-start(s8[5570560]{0:T(1024)(128)(4,1)} %bitcast.1), calls=%async_computation.1 | async-start | bytes 2752512
  17.0 9.3 %collective-permute-start.13 = (bf16[256,512]{1,0:T(8,128)(2,1)S(1)}, bf16[256,512]{1,0:T(8,128)(2,1)S(1)}, u32[]{:S(2)}, u32[]{:S(2)}) collective-permute-start(bf16[256,512]{1,0:T(8,128)(2,1)S(1)} %collective-permute-done.12.refs_4_), channel_id=1, source_target_pairs={{0,8},{4,12},{8,0},{12,4},{16,24},{20,28},{24,16},{28,20},{1,9},{5... | collective-permute-start | bytes 786440 | tf_op jit(solution)/shard_map/ppermute | solution.py:23
  17.8 9.7 %collective-permute-start.18 = (bf16[256,512]{1,0:T(8,128)(2,1)S(1)}, bf16[256,512]{1,0:T(8,128)(2,1)S(1)}, u32[]{:S(2)}, u32[]{:S(2)}) collective-permute-start(bf16[256,512]{1,0:T(8,128)(2,1)S(1)} %collective-permute-done.12.refs_4_), channel_id=1, source_target_pairs={{0,4},{4,0},{8,12},{12,8},{16,20},{20,16},{24,28},{28,24},{1,5},{5... | collective-permute-start | bytes 786440 | tf_op jit(solution)/shard_map/ppermute | solution.py:23
  19.3 13.3 %collective-permute-start.17 = (bf16[256,512]{1,0:T(8,128)(2,1)S(1)}, bf16[256,512]{1,0:T(8,128)(2,1)S(1)}, u32[]{:S(2)}, u32[]{:S(2)}) collective-permute-start(bf16[256,512]{1,0:T(8,128)(2,1)S(1)} %collective-permute-done.16.refs_2_), channel_id=1, source_target_pairs={{0,4},{4,0},{8,12},{12,8},{16,20},{20,16},{24,28},{28,24},{1,5},{5... | collective-permute-start | bytes 786440 | tf_op jit(solution)/shard_map/ppermute | solution.py:23
  19.8 2.0 %collective-permute-start.2 = (bf16[256,512]{1,0:T(8,128)(2,1)S(1)}, bf16[256,512]{1,0:T(8,128)(2,1)S(1)}, u32[]{:S(2)}, u32[]{:S(2)}) collective-permute-start(bf16[256,512]{1,0:T(8,128)(2,1)S(1)} %collective-permute-done.1.refs_2_), channel_id=1, source_target_pairs={{0,1},{1,0},{2,3},{3,2},{4,5},{5,4},{6,7},{7,6},{8,9},{9,8},{10,11... | collective-permute-start | bytes 786440 | tf_op jit(solution)/shard_map/ppermute | solution.py:23
  19.8 2.0 %copy-start = (bf16[256,512]{1,0:T(8,128)(2,1)S(1)}, bf16[256,512]{1,0:T(8,128)(2,1)}, u32[]{:S(2)}) copy-start(bf16[256,512]{1,0:T(8,128)(2,1)} %refs_4_.1) | copy-start | bytes 786436
  21.8 10.7 %copy-start.1 = (bf16[256,512]{1,0:T(8,128)(2,1)S(1)}, bf16[256,512]{1,0:T(8,128)(2,1)}, u32[]{:S(2)}) copy-start(bf16[256,512]{1,0:T(8,128)(2,1)} %refs_0_.5) | copy-start | bytes 786436
  24.3 24.7 %collective-permute-start.10 = (bf16[128,512]{1,0:T(8,128)(2,1)S(1)}, bf16[128,512]{1,0:T(8,128)(2,1)S(1)}, u32[]{:S(2)}, u32[]{:S(2)}) collective-permute-start(bf16[128,512]{1,0:T(8,128)(2,1)S(1)} %get-tuple-element.30), channel_id=1, source_target_pairs={{0,4},{4,0},{8,12},{12,8},{16,20},{20,16},{24,28},{28,24},{1,5},{5... | collective-permute-start | bytes 393224 | tf_op jit(solution)/shard_map/ppermute | solution.py:23
  26.2 24.1 %collective-permute-start.6 = (bf16[256,512]{1,0:T(8,128)(2,1)S(1)}, bf16[256,512]{1,0:T(8,128)(2,1)S(1)}, u32[]{:S(2)}, u32[]{:S(2)}) collective-permute-start(bf16[256,512]{1,0:T(8,128)(2,1)S(1)} %get-tuple-element.26), channel_id=1, source_target_pairs={{0,4},{4,0},{8,12},{12,8},{16,20},{20,16},{24,28},{28,24},{1,5},{5... | collective-permute-start | bytes 786440 | tf_op jit(solution)/shard_map/ppermute | solution.py:23
  26.4 19.6 %copy-start.2 = (bf16[128,512]{1,0:T(8,128)(2,1)S(1)}, bf16[128,512]{1,0:T(8,128)(2,1)}, u32[]{:S(2)}) copy-start(bf16[128,512]{1,0:T(8,128)(2,1)} %refs_6_.2) | copy-start | bytes 393220
  26.4 19.6 %copy-start.3 = (bf16[256,128]{1,0:T(8,128)(2,1)S(1)}, bf16[256,128]{1,0:T(8,128)(2,1)}, u32[]{:S(2)}) copy-start(bf16[256,128]{1,0:T(8,128)(2,1)} %refs_5_.2) | copy-start | bytes 196612
  26.4 27.4 %collective-permute-start.4 = (bf16[256,512]{1,0:T(8,128)(2,1)S(1)}, bf16[256,512]{1,0:T(8,128)(2,1)S(1)}, u32[]{:S(2)}, u32[]{:S(2)}) collective-permute-start(bf16[256,512]{1,0:T(8,128)(2,1)S(1)} %get-tuple-element.24), channel_id=1, source_target_pairs={{0,8},{4,12},{8,0},{12,4},{16,24},{20,28},{24,16},{28,20},{1,9},{5... | collective-permute-start | bytes 786440 | tf_op jit(solution)/shard_map/ppermute | solution.py:23
  27.5 17.9 %collective-permute-start.14 = (bf16[256,512]{1,0:T(8,128)(2,1)S(1)}, bf16[256,512]{1,0:T(8,128)(2,1)S(1)}, u32[]{:S(2)}, u32[]{:S(2)}) collective-permute-start(bf16[256,512]{1,0:T(8,128)(2,1)S(1)} %collective-permute-done.13.refs_6_), channel_id=1, source_target_pairs={{0,4},{4,0},{8,12},{12,8},{16,20},{20,16},{24,28},{28,24},{1,5},{5... | collective-permute-start | bytes 786440 | tf_op jit(solution)/shard_map/ppermute | solution.py:23
  45.8 31.2 %copy-start.7 = (bf16[256,256]{1,0:T(8,128)(2,1)S(1)}, bf16[256,256]{1,0:T(8,128)(2,1)}, u32[]{:S(2)}) copy-start(bf16[256,256]{1,0:T(8,128)(2,1)} %refs_3_.1) | copy-start | bytes 393220
  45.9 32.3 %copy-start.6 = (bf16[256,512]{1,0:T(8,128)(2,1)S(1)}, bf16[256,512]{1,0:T(8,128)(2,1)}, u32[]{:S(2)}) copy-start(bf16[256,512]{1,0:T(8,128)(2,1)} %refs_5_.3) | copy-start | bytes 786436
  45.9 9.2 %collective-permute-start.19 = (bf16[256,512]{1,0:T(8,128)(2,1)S(1)}, bf16[256,512]{1,0:T(8,128)(2,1)S(1)}, u32[]{:S(2)}, u32[]{:S(2)}) collective-permute-start(bf16[256,512]{1,0:T(8,128)(2,1)S(1)} %get-tuple-element.36), channel_id=1, source_target_pairs={{0,1},{1,0},{2,3},{3,2},{4,5},{5,4},{6,7},{7,6},{8,9},{9,8},{10,11... | collective-permute-start | bytes 786440 | tf_op jit(solution)/shard_map/ppermute | solution.py:23
  48.4 11.6 %collective-permute-start.3 = (bf16[256,512]{1,0:T(8,128)(2,1)S(1)}, bf16[256,512]{1,0:T(8,128)(2,1)S(1)}, u32[]{:S(2)}, u32[]{:S(2)}) collective-permute-start(bf16[256,512]{1,0:T(8,128)(2,1)S(1)} %get-tuple-element.22), channel_id=1, source_target_pairs={{0,8},{4,12},{8,0},{12,4},{16,24},{20,28},{24,16},{28,20},{1,9},{5... | collective-permute-start | bytes 786440 | tf_op jit(solution)/shard_map/ppermute | solution.py:23
  49.0 7.2 %collective-permute-start.8 = (bf16[128,512]{1,0:T(8,128)(2,1)S(1)}, bf16[128,512]{1,0:T(8,128)(2,1)S(1)}, u32[]{:S(2)}, u32[]{:S(2)}) collective-permute-start(bf16[128,512]{1,0:T(8,128)(2,1)S(1)} %get-tuple-element.28), channel_id=1, source_target_pairs={{0,4},{4,0},{8,12},{12,8},{16,20},{20,16},{24,28},{28,24},{1,5},{5... | collective-permute-start | bytes 393224 | tf_op jit(solution)/shard_map/ppermute | solution.py:23
  50.3 11.2 %collective-permute-start.11 = (bf16[128,512]{1,0:T(8,128)(2,1)S(1)}, bf16[128,512]{1,0:T(8,128)(2,1)S(1)}, u32[]{:S(2)}, u32[]{:S(2)}) collective-permute-start(bf16[128,512]{1,0:T(8,128)(2,1)S(1)} %join.7), channel_id=1, source_target_pairs={{0,16},{4,20},{8,24},{12,28},{16,0},{20,4},{24,8},{28,12},{1,17},{... | collective-permute-start | bytes 393224 | tf_op jit(solution)/shard_map/ppermute | solution.py:23
  53.7 23.3 %collective-permute-start.7 = (bf16[256,512]{1,0:T(8,128)(2,1)S(1)}, bf16[256,512]{1,0:T(8,128)(2,1)S(1)}, u32[]{:S(2)}, u32[]{:S(2)}) collective-permute-start(bf16[256,512]{1,0:T(8,128)(2,1)S(1)} %join.5), channel_id=1, source_target_pairs={{0,24},{4,28},{8,16},{12,20},{16,8},{20,12},{24,0},{28,4},{1,25},{... | collective-permute-start | bytes 786440 | tf_op jit(solution)/shard_map/ppermute | solution.py:23
  55.1 22.0 %collective-permute-start.5 = (bf16[256,512]{1,0:T(8,128)(2,1)S(1)}, bf16[256,512]{1,0:T(8,128)(2,1)S(1)}, u32[]{:S(2)}, u32[]{:S(2)}) collective-permute-start(bf16[256,512]{1,0:T(8,128)(2,1)S(1)} %join.4), channel_id=1, source_target_pairs={{0,4},{4,0},{8,12},{12,8},{16,20},{20,16},{24,28},{28,24},{1,5},{5... | collective-permute-start | bytes 786440 | tf_op jit(solution)/shard_map/ppermute | solution.py:23
  56.2 22.0 %collective-permute-start.20 = (bf16[256,512]{1,0:T(8,128)(2,1)S(1)}, bf16[256,512]{1,0:T(8,128)(2,1)S(1)}, u32[]{:S(2)}, u32[]{:S(2)}) collective-permute-start(bf16[256,512]{1,0:T(8,128)(2,1)S(1)} %get-tuple-element.38), channel_id=1, source_target_pairs={{0,1},{1,0},{2,3},{3,2},{4,5},{5,4},{6,7},{7,6},{8,9},{9,8},{10,11... | collective-permute-start | bytes 786440 | tf_op jit(solution)/shard_map/ppermute | solution.py:23
  60.0 18.1 %collective-permute-start.21 = (bf16[256,512]{1,0:T(8,128)(2,1)S(1)}, bf16[256,512]{1,0:T(8,128)(2,1)S(1)}, u32[]{:S(2)}, u32[]{:S(2)}) collective-permute-start(bf16[256,512]{1,0:T(8,128)(2,1)S(1)} %get-tuple-element.39), channel_id=1, source_target_pairs={{0,2},{1,3},{2,0},{3,1},{4,6},{5,7},{6,4},{7,5},{8,10},{9,11},{10,... | collective-permute-start | bytes 786440 | tf_op jit(solution)/shard_map/ppermute | solution.py:23
  61.5 15.5 %collective-permute-start.9 = (bf16[128,512]{1,0:T(8,128)(2,1)S(1)}, bf16[128,512]{1,0:T(8,128)(2,1)S(1)}, u32[]{:S(2)}, u32[]{:S(2)}) collective-permute-start(bf16[128,512]{1,0:T(8,128)(2,1)S(1)} %join.6), channel_id=1, source_target_pairs={{0,16},{4,20},{8,24},{12,28},{16,0},{20,4},{24,8},{28,12},{1,17},{... | collective-permute-start | bytes 393224 | tf_op jit(solution)/shard_map/ppermute | solution.py:23
